TPU v7x, 8 devices: a whole 2x2x1 slice. The times are simulated.
8 devices in a mesh: dp: 1 (over z), kv: 2 (over y), dup: 4 (over x, core).
Axes of the slice: x: 2, y: 2, z: 1, core: 2. Of those that a mesh axis runs over, the one named last changes fastest.
Arguments:
- query: bfloat16 [256, 32, 128], P('dp', ('kv', 'dup'))
- k_cache: bfloat16 [256, 2, 4096, 128], P('dp', 'kv')
- v_cache: bfloat16 [256, 2, 4096, 128], P('dp', 'kv')
- lengths: int32 [256], P('dp')
- w_out: bfloat16 [4096, 4096], P(('kv', 'dup'))
Outputs:
- output: bfloat16 [256, 4096], P('dp', ('kv', 'dup'))
All inputs are finite; a program needn't handle non-finite values.
Results may differ from a plain program's by a relative error of at most 0.00871299.
Values are sent between devices in bfloat16 or wider.
A program may use at most 2.25 GiB of HBM per device.

v0:
```python
import functools
import math

import jax
import jax.numpy as jnp
from jax import lax
from jax.experimental import pallas as pl
from jax.experimental.pallas import tpu as pltpu
from jax.sharding import PartitionSpec as P

R = 64
R1 = 32
R2 = R - R1
K2 = 4
T = 512
HT = T // 2
U = 8
NG = 7
NG2 = 6
G2 = R2 * K2 // U
G1 = R1 // U
PRE_LIMIT = 40 * 2**20
H = 16
D = 128
C = (D ** -0.5) * math.log2(math.e)
NEG = -3.0e38
MESH = pl.DeviceIdType.MESH
F32 = jnp.float32
BF16 = jnp.bfloat16


def _rcopy(src, dst, ssem, rsem, dev):
    return pltpu.make_async_remote_copy(src_ref=src, dst_ref=dst, send_sem=ssem, recv_sem=rsem,
                                        device_id=dev, device_id_type=MESH)


def _enter(peers):
    barrier = pltpu.get_barrier_semaphore()
    for p in peers:
        pl.semaphore_signal(barrier, inc=1, device_id=p, device_id_type=MESH)
    pl.semaphore_wait(barrier, len(peers))


def spread_kernel(q_ref, k_ref, v_ref, qr_ref, pre_ref, ssem, rsem, psem):
    me = lax.axis_index('dup')

    def load(r, c):
        for j, src in enumerate((k_ref, v_ref)):
            pltpu.make_async_copy(src.at[me * R + r, 0, pl.ds(0, T), :], pre_ref.at[r, j], psem).start()
        return c

    _enter([{'dup': lax.rem(me + k, 4)} for k in (1, 2, 3)])
    cps = []
    for k in (2, 1, 3):
        to = lax.rem(me + k, 4)
        cps.append(_rcopy(q_ref.at[pl.ds(to * R, R)], qr_ref.at[me], ssem.at[k - 1], rsem.at[k - 1], {'dup': to}))
    for c in cps:
        c.start()
    lax.fori_loop(0, R1, load, 0)
    for c in cps:
        c.wait()
    pltpu.make_async_copy(pre_ref, pre_ref, psem).wait()


def spread(q, k, v):
    any_ = pl.BlockSpec(memory_space=pltpu.HBM)
    dma = pltpu.SemaphoreType.DMA
    return pl.pallas_call(
        spread_kernel,
        out_shape=(pltpu.HBM((4, R, 4, D), BF16), pltpu.VMEM((R1, 2, T, D), BF16)),
        in_specs=[any_] * 3, out_specs=(any_, pl.BlockSpec(memory_space=pltpu.VMEM)),
        scratch_shapes=[dma((3,)), dma((3,)), dma],
        compiler_params=pltpu.CompilerParams(collective_id=0, has_side_effects=True, vmem_limit_bytes=PRE_LIMIT),
        name='spread',
    )(q, k, v)


def _side_by_side(ref):
    return jnp.concatenate([ref[0:HT, :], ref[HT:T, :]], axis=1)


def _scores(q, k):
    q16 = q.astype(BF16)
    z16 = jnp.zeros_like(q16)
    q2 = jnp.concatenate([jnp.concatenate([q16, z16], 1), jnp.concatenate([z16, q16], 1)], 0)
    return lax.dot_general(q2, _side_by_side(k), (((1,), (1,)), ((), ())), preferred_element_type=F32)


def _weighted(p, v):
    o2 = jnp.dot(p, _side_by_side(v), preferred_element_type=F32)
    return o2[0:H, 0:D] + o2[H:, D:]


def _positions():
    half = lax.broadcasted_iota(jnp.int32, (2 * H, HT), 0) // H
    return half * HT + lax.broadcasted_iota(jnp.int32, (2 * H, HT), 1)


def _softmax(s, pos, rem, pbuf, mbuf, lbuf):
    s = jnp.where(pos < rem, s, NEG)
    m = jnp.max(jnp.maximum(s[0:H], s[H:]), axis=1, keepdims=True)
    p = jnp.exp2((s - jnp.concatenate([m, m], 0)) * C)
    pbuf[...] = p.astype(BF16)
    mbuf[...] = jnp.broadcast_to(m, (H, D))
    lbuf[...] = jnp.broadcast_to(jnp.sum(p[0:H] + p[H:], axis=1, keepdims=True), (H, D))


def _merge(state, m, l, acc):
    m0, l0, a0 = state
    mn = jnp.maximum(m0, m)
    a = jnp.exp2((m0 - mn) * C)
    c = jnp.exp2((m - mn) * C)
    return mn, l0 * a + l * c, a0 * a + acc * c


def attn_kernel(len_ref, q_own, q_recv, pre, k_ref, v_ref, o_ref, st_ref, q2_ref,
                qv, q32, kv, sbuf, pbuf, mbuf, lbuf, o32, l32, m32, oi, li, mi, rows, tbl, qsem, sem):
    base = lax.axis_index('dup') * R
    me = lax.axis_index('dup')
    qcp = [pltpu.make_async_copy(q_recv.at[lax.rem(me + k, 4)], qv.at[lax.rem(me + k, 4)], qsem.at[k]) for k in range(1, 4)]
    qcp.append(pltpu.make_async_copy(q_own.at[pl.ds(base, R)], qv.at[me], qsem.at[0]))
    for c in qcp:
        c.start()

    def first_tile(row):
        return jnp.where(row < R1, 1, K2)

    def count(i, c):
        cnt, n = c
        items = jnp.maximum((len_ref[base + i] + T - 1) // T - first_tile(i), 0)
        rows[cnt] = i
        return cnt + jnp.where(items > 0, 1, 0), n + items

    cnt, n = lax.fori_loop(0, R, count, (jnp.int32(0), jnp.int32(0)), unroll=4)
    rows[cnt] = R
    ng = (n + U - 1) // U

    def plan(b, st):
        k, tile = st
        for u in range(U):
            row = rows[k]
            live = row < R
            length = len_ref[base + jnp.minimum(row, R - 1)]
            t = jnp.where(live, tile, 0)
            tbl[0, b * U + u] = row
            tbl[1, b * U + u] = jnp.where(live, length - t * T, 0)
            tbl[2, b * U + u] = t
            done = jnp.logical_and((tile + 1) * T >= length, live)
            k = jnp.where(done, k + 1, k)
            tile = jnp.where(done, first_tile(rows[k]), tile + 1)
        return k, tile

    def issue(b):
        for u in range(U):
            row = base + jnp.minimum(tbl[0, b * U + u], R - 1)
            at = pl.ds(pl.multiple_of(tbl[2, b * U + u] * T, T), T)
            pltpu.make_async_copy(k_ref.at[row, 0, at, :], kv.at[b, u, 0], sem.at[b]).start()
            pltpu.make_async_copy(v_ref.at[row, 0, at, :], kv.at[b, u, 1], sem.at[b]).start()

    def fetch_group(b, st):
        st = plan(b, st)
        issue(b)
        return st

    def wait_group(b):
        pltpu.make_async_copy(kv.at[b], kv.at[b], sem.at[b]).wait()

    z = jnp.int32(0)
    pst = lax.fori_loop(0, jnp.minimum(3, ng), fetch_group, (z, first_tile(rows[0])))

    for dst, val in ((m32, NEG), (l32, 0.0), (o32, 0.0), (mi, NEG), (li, 0.0), (oi, 0.0)):
        dst[pl.ds(R1 * H, R2 * H + H), :] = jnp.full((R2 * H + H, D), val, F32)
    for c in qcp:
        c.wait()
    for s in range(4):
        q32[0:R, 4 * s:4 * s + 4, :] = qv[s].astype(F32)

    q2_ref[...] = q32[R1:R]
    pst = lax.fori_loop(jnp.minimum(3, ng), jnp.minimum(NG, ng), fetch_group, pst)

    pos = _positions()
    def lead(g):
        cur, oth = g % 2, 1 - g % 2
        accs = [_weighted(pbuf[oth, u], pre.at[(g - 1) * U + u, 1]) for u in range(U)] if g else None
        return cur, oth, accs

    def store(g, oth, accs):
        for u in range(U):
            at = pl.ds((g * U + u) * H, H)
            for dst, dst2, val in ((m32, mi, mbuf[oth, u]), (l32, li, lbuf[oth, u]), (o32, oi, accs[u])):
                dst[at, :] = val
                dst2[at, :] = val

    def next_scores(g, oth):
        nb = lax.rem(g, NG)
        for u in range(U):
            sbuf[oth, u] = _scores(q32[jnp.where(g < ng, tbl[0, nb * U + u], 0)], kv.at[nb, u, 0])

    def softmax(cur, rems):
        for u in range(U):
            _softmax(sbuf[cur, u], pos, rems[u], pbuf.at[cur, u], mbuf.at[cur, u], lbuf.at[cur, u])

    for u in range(U):
        sbuf[0, u] = _scores(q32[u], pre.at[u, 0])
    for g in range(G1):
        cur, oth, accs = lead(g)
        if g + 1 < G1:
            for u in range(U):
                sbuf[oth, u] = _scores(q32[(g + 1) * U + u], pre.at[(g + 1) * U + u, 0])
        else:
            @pl.when(ng > 0)
            def _():
                wait_group(0)
            next_scores(jnp.int32(0), oth)
        softmax(cur, [len_ref[base + g * U + u] for u in range(U)])
        if g:
            store(g - 1, oth, accs)
    @pl.when(ng > 1)
    def _():
        wait_group(1)
    accs = [_weighted(pbuf[1, u], pre.at[(G1 - 1) * U + u, 1]) for u in range(U)]
    next_scores(jnp.int32(1), 1)
    softmax(0, [jnp.where(ng > 0, tbl[1, u], 0) for u in range(U)])
    store(G1 - 1, 1, accs)

    def stage(g, cur, carry):
        pst, state = carry
        oth = 1 - cur
        bp = lax.rem(g - 1, NG)
        b = lax.rem(g, NG)
        nb = lax.rem(g + 1, NG)

        @pl.when(g + 1 < ng)
        def _():
            wait_group(nb)
        accs = [_weighted(pbuf[oth, u], kv.at[bp, u, 1]) for u in range(U)]
        next_scores(g + 1, oth)
        softmax(cur, [jnp.where(g < ng, tbl[1, b * U + u], 0) for u in range(U)])
        for u in range(U):
            row = jnp.where(g - 1 < ng, tbl[0, bp * U + u], R)
            at = pl.ds(pl.multiple_of(row * H, H), H)
            first = tbl[2, bp * U + u] == first_tile(row)
            state = tuple(jnp.where(first, src[at, :], val) for src, val in zip((mi, li, oi), state))
            state = _merge(state, mbuf[oth, u], lbuf[oth, u], accs[u])
            for dst, val in zip((m32, l32, o32), state):
                dst[at, :] = val
        more = g - 1 + NG < ng
        slot = jnp.where(more, bp, NG)
        nst = plan(slot, pst)
        @pl.when(more)
        def _():
            issue(bp)
        return (jnp.where(more, nst[0], pst[0]), jnp.where(more, nst[1], pst[1])), state

    def body(h, carry):
        return stage(2 * h + 2, 0, stage(2 * h + 1, 1, carry))

    state = (jnp.full((H, D), NEG, F32), jnp.ones((H, D), F32), jnp.zeros((H, D), F32))
    lax.fori_loop(0, (ng + 1) // 2, body, (pst, state))
    for i, src in enumerate((m32, l32, o32)):
        st_ref[i] = src[pl.ds(R1 * H, R2 * H), :]
    for h in range(H):
        o_ref[h] = (o32[pl.ds(h, R1, stride=H), :] / l32[pl.ds(h, R1, stride=H), :]).astype(BF16)


def attention(q_own, q_recv, pre, k, v, lens):
    any_ = pl.BlockSpec(memory_space=pltpu.HBM)
    dma = pltpu.SemaphoreType.DMA
    return pl.pallas_call(
        attn_kernel,
        out_shape=(pltpu.VMEM((H, R1, D), BF16), pltpu.VMEM((3, R2 * H, D), F32), pltpu.VMEM((R2, H, D), F32)),
        in_specs=[pl.BlockSpec(memory_space=pltpu.SMEM), any_, any_, pl.BlockSpec(memory_space=pltpu.VMEM), any_, any_],
        out_specs=(pl.BlockSpec(memory_space=pltpu.VMEM),) * 3,
        scratch_shapes=[
            pltpu.VMEM((4, R, 4, D), BF16), pltpu.VMEM((R + 1, H, D), F32),
            pltpu.VMEM((NG, U, 2, T, D), BF16),
            pltpu.VMEM((2, U, 2 * H, HT), F32), pltpu.VMEM((2, U, 2 * H, HT), BF16),
            pltpu.VMEM((2, U, H, D), F32), pltpu.VMEM((2, U, H, D), F32),
            *[pltpu.VMEM(((R + 1) * H, D), F32)] * 6,
            pltpu.SMEM((R + 1,), jnp.int32), pltpu.SMEM((3, (NG + 1) * U), jnp.int32),
            dma((4,)), dma((NG,)),
        ],
        compiler_params=pltpu.CompilerParams(vmem_limit_bytes=PRE_LIMIT),
        name='attn',
    )(lens, q_own, q_recv, pre, k, v)


def tail_kernel(len_ref, o1_ref, st_ref, qt, k_ref, v_ref, w_ref, y_ref,
                st, kv, sbuf, pbuf, mbuf, lbuf, o2v, oc, wv, part, r1a, r1b, r2a, r2b,
                sem, wsem, wss, wsr, oss, osr, s1s, s1a, s1b, s2s, s2a, s2b):
    me = lax.axis_index('dup')
    kvi = lax.axis_index('kv')
    core = lax.rem(me, 2)
    x = me // 2
    ox, okv = 1 - x, 1 - kvi
    mate = me + 1 - 2 * core
    far = lax.rem(me + 2, 4)
    to_mate, to_x, to_y = {'dup': mate}, {'dup': far}, {'kv': okv}
    base = me * R + R1
    RR = R1

    def fetch_group(g):
        b = lax.rem(g, NG2)
        for u in range(U):
            i = g * U + u
            for j, src in enumerate((k_ref, v_ref)):
                pltpu.make_async_copy(src.at[base + i // K2, 0, pl.ds(pl.multiple_of(lax.rem(i, K2) * T, T), T), :],
                                      kv.at[b, u, j], sem.at[b]).start()

    def wait_group(g):
        b = lax.rem(g, NG2)
        pltpu.make_async_copy(kv.at[b], kv.at[b], sem.at[b]).wait()

    for g in range(2):
        fetch_group(jnp.int32(g))
    _enter([to_mate, to_x, to_y])

    def exchange(p, src):
        o_x = _rcopy(src.at[pl.ds(ox * 8, 8)], oc.at[p, me], oss.at[p, 0], osr.at[p, 0], to_x)
        o_m = _rcopy(src.at[pl.ds(x * 8, 8)], oc.at[p, me], oss.at[p, 1], osr.at[p, 1], to_mate)
        o_x.start()
        o_m.start()
        return o_x, o_m

    o_x, o_m = exchange(0, o1_ref)
    oc[0, me] = o1_ref[pl.ds(x * 8, 8)]
    order = (okv * 2 + ox, kvi * 2 + ox, okv * 2 + x, kvi * 2 + x)
    wcps = []
    for i, j in enumerate(order):
        here = pl.multiple_of((j * 2 + core) * 512, 512)
        there = pl.multiple_of((j * 2 + 1 - core) * 512, 512)
        mine = wv.at[j, pl.ds(pl.multiple_of(core * 512, 512), 512)]
        wcps.append(pltpu.make_async_copy(w_ref.at[:, pl.ds(here, 512)], mine, wsem.at[i]))
        wcps.append(_rcopy(w_ref.at[:, pl.ds(there, 512)], mine, wss.at[j], wsr.at[j], to_mate))
    for c in wcps:
        c.start()
    for g in range(2, NG2):
        fetch_group(jnp.int32(g))

    pos = _positions()
    sends = []

    def forward(p, o_x):
        o_x.wait()
        fwd = _rcopy(oc.at[p, far], oc.at[p, far], oss.at[p, 2], osr.at[p, 2], to_mate)
        fwd.start()
        return fwd

    def multiply(p, ts):
        Xs = [x if t == 0 else ox for t in ts]
        lhs = jnp.concatenate(
            [jnp.concatenate([oc[p, 2 * X + c, h] for X in Xs for c in range(2)], axis=0) for h in range(8)], axis=1)
        M = 2 * RR
        for j in order:
            out = jnp.dot(lhs, wv[j], preferred_element_type=F32)
            for n, X in enumerate(Xs):
                part[p, X, j, 0] = out[n * M:(n + 1) * M, :256]
                part[p, X, j, 1] = out[n * M:(n + 1) * M, 256:]
        for t, X in zip(ts, Xs):
            for i, j in enumerate(order):
                if i in (0, 1):
                    k = okv if i == 0 else kvi
                    sends.append(_rcopy(part.at[p, X, j, 0], r1a.at[p, X, k], s1s.at[p, t, 2 * i], s1a.at[p, X, k], to_x))
                    sends[-1].start()
                if i in (0, 2):
                    xx = ox if i == 0 else x
                    sends.append(_rcopy(part.at[p, X, j, 1], r1b.at[p, X, xx], s1s.at[p, t, i + 1], s1b.at[p, X, xx], to_y))
                    sends[-1].start()

    def arrived(dst, rsem, dev):
        _rcopy(dst, dst, s1s.at[0, 0, 0], rsem, dev).wait_recv()

    jm = kvi * 2 + x

    def second(p):
        for t in range(2):
            Xa = ox if t == 0 else x
            Xb = x if t == 0 else ox
            ja = okv * 2 + x
            arrived(r1a.at[p, Xa, okv], s1a.at[p, Xa, okv], to_x)
            part[p, Xa, ja, 0] = part[p, Xa, ja, 0] + r1a[p, Xa, okv]
            sends.append(_rcopy(part.at[p, Xa, ja, 0], r2a.at[p, Xa], s2s.at[p, t, 0], s2a.at[p, Xa], to_y))
            sends[-1].start()
            jb = kvi * 2 + ox
            arrived(r1b.at[p, Xb, ox], s1b.at[p, Xb, ox], to_y)
            part[p, Xb, jb, 1] = part[p, Xb, jb, 1] + r1b[p, Xb, ox]
            sends.append(_rcopy(part.at[p, Xb, jb, 1], r2b.at[p, Xb], s2s.at[p, t, 1], s2b.at[p, Xb], to_x))
            sends[-1].start()
            arrived(r1a.at[p, Xa, kvi], s1a.at[p, Xa, kvi], to_x)
            part[p, Xa, jm, 0] = part[p, Xa, jm, 0] + r1a[p, Xa, kvi]
            arrived(r1b.at[p, Xb, x], s1b.at[p, Xb, x], to_y)
            part[p, Xb, jm, 1] = part[p, Xb, jm, 1] + r1b[p, Xb, x]

    def finish(p):
        for t in range(2):
            X = ox if t == 0 else x
            arrived(r2a.at[p, X], s2a.at[p, X], to_y)
            arrived(r2b.at[p, X], s2b.at[p, X], to_x)
            for half, r in ((0, r2a), (1, r2b)):
                val = (part[p, X, jm, half] + r[p, X]).astype(BF16)
                for c in range(2):
                    row = pl.multiple_of(X * 2 * R + c * R + p * RR, RR)
                    y_ref[pl.ds(row, RR), half * 256:half * 256 + 256] = val[c * RR:(c + 1) * RR]

    def scores(g, oth):
        b = lax.rem(g, NG2)
        for u in range(U):
            sbuf[oth, u] = _scores(qt[(g * U + u) // K2], kv.at[b, u, 0])

    def stage(g, cur, state, qk=True, sm=True, pv=True):
        oth = 1 - cur
        if qk:
            wait_group(g + 1)
        accs = None
        bp = lax.rem(g - 1 + NG2, NG2)
        if pv:
            accs = [_weighted(pbuf[oth, u], kv.at[bp, u, 1]) for u in range(U)]
        if qk:
            scores(g + 1, oth)
        if sm:
            for u in range(U):
                i = g * U + u
                rem = len_ref[base + i // K2] - lax.rem(i, K2) * T
                _softmax(sbuf[cur, u], pos, rem, pbuf.at[cur, u], mbuf.at[cur, u], lbuf.at[cur, u])
        if pv:
            for u in range(U):
                i = (g - 1) * U + u
                at = pl.ds(pl.multiple_of((i // K2) * H, H), H)
                if u % K2 == 0:
                    state = (st_ref[0, at, :], st_ref[1, at, :], st_ref[2, at, :])
                state = _merge(state, mbuf[oth, u], lbuf[oth, u], accs[u])
                if u % K2 == K2 - 1:
                    st[0, at, :] = state[1]
                    st[1, at, :] = state[2]
        if qk and pv:
            @pl.when(g - 1 + NG2 < G2)
            def _():
                fetch_group(g - 1 + NG2)
        return state

    def pair(h, state):
        return stage(2 * h + 2, 0, stage(2 * h + 1, 1, state))

    wait_group(jnp.int32(0))
    scores(jnp.int32(0), 0)
    state = (jnp.zeros((H, D), F32),) * 3
    stage(jnp.int32(0), 0, state, pv=False)
    last = (G2 - 2) // 2
    state = lax.fori_loop(0, 1, pair, state)
    fwd = forward(0, o_x)
    state = lax.fori_loop(1, 2, pair, state)
    fwd.wait()
    o_m.wait()
    for c in wcps:
        c.wait()
    multiply(0, (0, 1))
    state = lax.fori_loop(2, last, pair, state)
    stage(jnp.int32(G2 - 1), 1, state, qk=False)
    stage(jnp.int32(G2), 0, state, qk=False, sm=False)
    for h in range(H):
        o2v[h] = (st[1, pl.ds(h, R2, stride=H), :] / st[0, pl.ds(h, R2, stride=H), :]).astype(BF16)
    o_x, o_m = exchange(1, o2v)
    oc[1, me] = o2v[pl.ds(x * 8, 8)]
    o_m.wait()
    multiply(1, (0,))
    second(0)
    fwd = forward(1, o_x)
    finish(0)
    fwd.wait()
    multiply(1, (1,))
    second(1)
    finish(1)
    for c in sends:
        c.wait_send()


def tail(lens, o1, st, q2, k, v, w):
    any_ = pl.BlockSpec(memory_space=pltpu.HBM)
    dma = pltpu.SemaphoreType.DMA
    M = 2 * R1
    return pl.pallas_call(
        tail_kernel,
        out_shape=jax.ShapeDtypeStruct((256, 512), BF16),
        in_specs=[pl.BlockSpec(memory_space=pltpu.SMEM)] + [pl.BlockSpec(memory_space=pltpu.VMEM)] * 3 + [any_] * 3, out_specs=pl.BlockSpec(memory_space=pltpu.VMEM),
        scratch_shapes=[
            pltpu.VMEM((2, R2 * H, D), F32),
            pltpu.VMEM((NG2, U, 2, T, D), BF16),
            pltpu.VMEM((2, U, 2 * H, HT), F32), pltpu.VMEM((2, U, 2 * H, HT), BF16),
            pltpu.VMEM((2, U, H, D), F32), pltpu.VMEM((2, U, H, D), F32),
            pltpu.VMEM((H, R2, D), BF16),
            pltpu.VMEM((2, 4, 8, R1, D), BF16), pltpu.VMEM((4, 1024, 512), BF16),
            pltpu.VMEM((2, 2, 4, 2, M, 256), F32),
            pltpu.VMEM((2, 2, 2, M, 256), F32), pltpu.VMEM((2, 2, 2, M, 256), F32),
            pltpu.VMEM((2, 2, M, 256), F32), pltpu.VMEM((2, 2, M, 256), F32),
            dma((NG2,)), dma((4,)), dma((4,)), dma((4,)), dma((2, 3)), dma((2, 3)),
            dma((2, 2, 4)), dma((2, 2, 2)), dma((2, 2, 2)),
            dma((2, 2, 2)), dma((2, 2)), dma((2, 2)),
        ],
        compiler_params=pltpu.CompilerParams(collective_id=1, has_side_effects=True, vmem_limit_bytes=52 * 2**20),
        name='tail',
    )(lens, o1, st, q2, k, v, w)


def solution(mesh):
    def per_device(q, k, v, lens, w):
        q, lens, w = (pltpu.with_memory_space_constraint(a, pltpu.HBM) for a in (q, lens, w))
        q_recv, pre = spread(q, k, v)
        q_recv = pltpu.with_memory_space_constraint(q_recv, pltpu.HBM)
        o1, st, q2 = attention(q, q_recv, pre, k, v, lens)
        return tail(lens, o1, st, q2, k, v, w)

    return jax.shard_map(
        per_device,
        mesh=mesh,
        in_specs=(P('dp', ('kv', 'dup'), None), P('dp', 'kv', None, None), P('dp', 'kv', None, None), P('dp'), P(('kv', 'dup'), None)),
        out_specs=P('dp', ('kv', 'dup')),
        check_vma=False,
    )
```

profile of v0, /device:TPU:0, one launch (start us, length us, event | category | flops | bytes accessed | tf_op | source)
XLA Modules:
  0.0 61.9 jit_solution(7391992902604085728)
XLA Ops:
  0.0 7.4 %spread.1 = (bf16[4,64,4,128]{3,2,1,0:T(4,128)(2,1)}, bf16[32,2,512,128]{3,2,1,0:T(8,128)(2,1)S(1)}) custom-call(bf16[256,4,128]{2,1,0:T(4,128)(2,1)} %q_own.1, bf16[256,1,4096,128]{3,2,1,0:T(8,128)(2,1)} %k_ref.5, bf16[256,1,4096,128]{3,2,1,0:T(8,128)(2,1)} %v_ref.5), custom_call_target="tpu_custom_call" | custom-call | tf_op jit(solution)/shard_map/spread/pallas_call | solution.py:68
  7.4 20.1 %attn.1 = (bf16[16,32,128]{2,1,0:T(8,128)(2,1)S(1)}, f32[3,512,128]{2,1,0:T(8,128)S(1)}, f32[32,16,128]{2,1,0:T(8,128)S(1)}) custom-call(s32[256]{0:T(256)} %len_ref.3, bf16[256,4,128]{2,1,0:T(4,128)(2,1)} %q_own.1, bf16[4,64,4,128]{3,2,1,0:T(4,128)(2,1)} %get-tuple-element.10.q_recv, bf16[32,2,512,128]{3,2,1,0:T(8,128)(2,1)S(1)} %get-tuple-element.11.pre, ...), custom_call_target="tpu_custom_call" | custom-call | tf_op jit(solution)/shard_map/attn/pallas_call | solution.py:269
  27.5 33.7 %tail.1 = bf16[256,512]{1,0:T(8,128)(2,1)S(1)} custom-call(s32[256]{0:T(256)} %len_ref.3, bf16[16,32,128]{2,1,0:T(8,128)(2,1)S(1)} %get-tuple-element.12.o1_ref, f32[3,512,128]{2,1,0:T(8,128)S(1)} %get-tuple-element.13.st_ref, f32[32,16,128]{2,1,0:T(8,128)S(1)} %get-tuple-element.14.qt, bf16[256,1,4096,128]{3,2,1,0:T(8,128)(2,1)} %k_ref.5, ...), custom_call_target="tpu_custom_call" | custom-call | tf_op jit(solution)/shard_map/tail/pallas_call | solution.py:481
  61.2 0.7 %copy.7 = bf16[256,512]{1,0:T(8,128)(2,1)} copy(bf16[256,512]{1,0:T(8,128)(2,1)S(1)} %tail.1) | data formatting | bytes 524288
where the time goes:
time: 61.9 us
  Pallas kernels  61.2 us (99%)
  local copies, waits for them, and re-layouts  0.71 us (1%)
    pallas_call x1, Pallas kernels, tail(): pl.pallas_call(tail_kernel, out_shape=jax.ShapeDtypeStruct((256, 512), BF...  33.7 us
    pallas_call x1, Pallas kernels, attention(): pl.pallas_call(attn_kernel, out_shape=(pltpu.VMEM((H, R1, D), BF16), pltp...  20.1 us
    pallas_call x1, Pallas kernels, spread(): pl.pallas_call(spread_kernel, out_shape=(pltpu.HBM((4, R, 4, D), BF16), p...  7.39 us

commit v1 on v0

--- a/solution.py
+++ b/solution.py
@@ -41,8 +41,10 @@
     pl.semaphore_wait(barrier, len(peers))
 
 
-def spread_kernel(q_ref, k_ref, v_ref, qr_ref, pre_ref, ssem, rsem, psem):
+def spread_kernel(q_ref, w_ref, k_ref, v_ref, qr_ref, pre_ref, wv_ref, ssem, rsem, wsem, wss, wsr, psem):
     me = lax.axis_index('dup')
+    core = lax.rem(me, 2)
+    mate = me + 1 - 2 * core
 
     def load(r, c):
         for j, src in enumerate((k_ref, v_ref)):
@@ -54,6 +56,12 @@
     for k in (2, 1, 3):
         to = lax.rem(me + k, 4)
         cps.append(_rcopy(q_ref.at[pl.ds(to * R, R)], qr_ref.at[me], ssem.at[k - 1], rsem.at[k - 1], {'dup': to}))
+    for j in range(4):
+        here = pl.multiple_of((j * 2 + core) * 512, 512)
+        there = pl.multiple_of((j * 2 + 1 - core) * 512, 512)
+        mine = wv_ref.at[j, pl.ds(pl.multiple_of(core * 512, 512), 512)]
+        cps.append(_rcopy(w_ref.at[:, pl.ds(there, 512)], mine, wss.at[j], wsr.at[j], {'dup': mate}))
+        cps.append(pltpu.make_async_copy(w_ref.at[:, pl.ds(here, 512)], mine, wsem.at[j]))
     for c in cps:
         c.start()
     lax.fori_loop(0, R1, load, 0)
@@ -62,17 +70,18 @@
     pltpu.make_async_copy(pre_ref, pre_ref, psem).wait()
 
 
-def spread(q, k, v):
+def spread(q, w, k, v):
     any_ = pl.BlockSpec(memory_space=pltpu.HBM)
     dma = pltpu.SemaphoreType.DMA
     return pl.pallas_call(
         spread_kernel,
-        out_shape=(pltpu.HBM((4, R, 4, D), BF16), pltpu.VMEM((R1, 2, T, D), BF16)),
-        in_specs=[any_] * 3, out_specs=(any_, pl.BlockSpec(memory_space=pltpu.VMEM)),
-        scratch_shapes=[dma((3,)), dma((3,)), dma],
+        out_shape=(pltpu.HBM((4, R, 4, D), BF16), pltpu.VMEM((R1, 2, T, D), BF16),
+                   pltpu.VMEM((4, 1024, 512), BF16)),
+        in_specs=[any_] * 4, out_specs=(any_,) + (pl.BlockSpec(memory_space=pltpu.VMEM),) * 2,
+        scratch_shapes=[dma((3,)), dma((3,)), dma((4,)), dma((4,)), dma((4,)), dma],
         compiler_params=pltpu.CompilerParams(collective_id=0, has_side_effects=True, vmem_limit_bytes=PRE_LIMIT),
         name='spread',
-    )(q, k, v)
+    )(q, w, k, v)
 
 
 def _side_by_side(ref):
@@ -285,9 +294,9 @@
     )(lens, q_own, q_recv, pre, k, v)
 
 
-def tail_kernel(len_ref, o1_ref, st_ref, qt, k_ref, v_ref, w_ref, y_ref,
-                st, kv, sbuf, pbuf, mbuf, lbuf, o2v, oc, wv, part, r1a, r1b, r2a, r2b,
-                sem, wsem, wss, wsr, oss, osr, s1s, s1a, s1b, s2s, s2a, s2b):
+def tail_kernel(len_ref, o1_ref, st_ref, qt, wv, k_ref, v_ref, y_ref,
+                st, kv, sbuf, pbuf, mbuf, lbuf, o2v, oc, part, r1a, r1b, r2a, r2b,
+                sem, oss, osr, s1s, s1a, s1b, s2s, s2a, s2b):
     me = lax.axis_index('dup')
     kvi = lax.axis_index('kv')
     core = lax.rem(me, 2)
@@ -325,15 +334,6 @@
     o_x, o_m = exchange(0, o1_ref)
     oc[0, me] = o1_ref[pl.ds(x * 8, 8)]
     order = (okv * 2 + ox, kvi * 2 + ox, okv * 2 + x, kvi * 2 + x)
-    wcps = []
-    for i, j in enumerate(order):
-        here = pl.multiple_of((j * 2 + core) * 512, 512)
-        there = pl.multiple_of((j * 2 + 1 - core) * 512, 512)
-        mine = wv.at[j, pl.ds(pl.multiple_of(core * 512, 512), 512)]
-        wcps.append(pltpu.make_async_copy(w_ref.at[:, pl.ds(here, 512)], mine, wsem.at[i]))
-        wcps.append(_rcopy(w_ref.at[:, pl.ds(there, 512)], mine, wss.at[j], wsr.at[j], to_mate))
-    for c in wcps:
-        c.start()
     for g in range(2, NG2):
         fetch_group(jnp.int32(g))
 
@@ -451,8 +451,6 @@
     state = lax.fori_loop(1, 2, pair, state)
     fwd.wait()
     o_m.wait()
-    for c in wcps:
-        c.wait()
     multiply(0, (0, 1))
     state = lax.fori_loop(2, last, pair, state)
     stage(jnp.int32(G2 - 1), 1, state, qk=False)
@@ -474,40 +472,40 @@
         c.wait_send()
 
 
-def tail(lens, o1, st, q2, k, v, w):
+def tail(lens, o1, st, q2, wv, k, v):
     any_ = pl.BlockSpec(memory_space=pltpu.HBM)
     dma = pltpu.SemaphoreType.DMA
     M = 2 * R1
     return pl.pallas_call(
         tail_kernel,
         out_shape=jax.ShapeDtypeStruct((256, 512), BF16),
-        in_specs=[pl.BlockSpec(memory_space=pltpu.SMEM)] + [pl.BlockSpec(memory_space=pltpu.VMEM)] * 3 + [any_] * 3, out_specs=pl.BlockSpec(memory_space=pltpu.VMEM),
+        in_specs=[pl.BlockSpec(memory_space=pltpu.SMEM)] + [pl.BlockSpec(memory_space=pltpu.VMEM)] * 4 + [any_] * 2, out_specs=pl.BlockSpec(memory_space=pltpu.VMEM),
         scratch_shapes=[
             pltpu.VMEM((2, R2 * H, D), F32),
             pltpu.VMEM((NG2, U, 2, T, D), BF16),
             pltpu.VMEM((2, U, 2 * H, HT), F32), pltpu.VMEM((2, U, 2 * H, HT), BF16),
             pltpu.VMEM((2, U, H, D), F32), pltpu.VMEM((2, U, H, D), F32),
             pltpu.VMEM((H, R2, D), BF16),
-            pltpu.VMEM((2, 4, 8, R1, D), BF16), pltpu.VMEM((4, 1024, 512), BF16),
+            pltpu.VMEM((2, 4, 8, R1, D), BF16),
             pltpu.VMEM((2, 2, 4, 2, M, 256), F32),
             pltpu.VMEM((2, 2, 2, M, 256), F32), pltpu.VMEM((2, 2, 2, M, 256), F32),
             pltpu.VMEM((2, 2, M, 256), F32), pltpu.VMEM((2, 2, M, 256), F32),
-            dma((NG2,)), dma((4,)), dma((4,)), dma((4,)), dma((2, 3)), dma((2, 3)),
+            dma((NG2,)), dma((2, 3)), dma((2, 3)),
             dma((2, 2, 4)), dma((2, 2, 2)), dma((2, 2, 2)),
             dma((2, 2, 2)), dma((2, 2)), dma((2, 2)),
         ],
-        compiler_params=pltpu.CompilerParams(collective_id=1, has_side_effects=True, vmem_limit_bytes=52 * 2**20),
+        compiler_params=pltpu.CompilerParams(collective_id=1, has_side_effects=True, vmem_limit_bytes=48 * 2**20),
         name='tail',
-    )(lens, o1, st, q2, k, v, w)
+    )(lens, o1, st, q2, wv, k, v)
 
 
 def solution(mesh):
     def per_device(q, k, v, lens, w):
         q, lens, w = (pltpu.with_memory_space_constraint(a, pltpu.HBM) for a in (q, lens, w))
-        q_recv, pre = spread(q, k, v)
+        q_recv, pre, wv = spread(q, w, k, v)
         q_recv = pltpu.with_memory_space_constraint(q_recv, pltpu.HBM)
         o1, st, q2 = attention(q, q_recv, pre, k, v, lens)
-        return tail(lens, o1, st, q2, k, v, w)
+        return tail(lens, o1, st, q2, wv, k, v)
 
     return jax.shard_map(
         per_device,

time: 61.9 us -> 61 us (0.985)
  Pallas kernels: 61.2 us -> 60.1 us
    pallas_call x1, Pallas kernels: 20.1 us -> 17.4 us  [attention(): pl.pallas_call(attn_kernel, out_shape=(pltpu.VMEM((H, R1, D), BF16), pltp...]
    pallas_call x1, Pallas kernels: 33.7 us -> 35.2 us  [tail(): pl.pallas_call(tail_kernel, out_shape=jax.ShapeDtypeStruct((256, 512), BF...]
where the time goes in v1:
time: 61 us; the launch traced here: 60.8 us
  Pallas kernels  60.1 us (99%)
  local copies, waits for them, and re-layouts  0.71 us (1%)
    pallas_call x1, Pallas kernels, tail(): pl.pallas_call(tail_kernel, out_shape=jax.ShapeDtypeStruct((256, 512), BF...  35.2 us
    pallas_call x1, Pallas kernels, attention(): pl.pallas_call(attn_kernel, out_shape=(pltpu.VMEM((H, R1, D), BF16), pltp...  17.4 us
    pallas_call x1, Pallas kernels, spread(): pl.pallas_call(spread_kernel, out_shape=(pltpu.HBM((4, R, 4, D), BF16), p...  7.52 us

profile of v1, /device:TPU:0, one launch (start us, length us, event | category | flops | bytes accessed | tf_op | source)
XLA Modules:
  0.0 60.8 jit_solution(12386151088531231827)
XLA Ops:
  0.0 7.5 %spread.1 = (bf16[4,64,4,128]{3,2,1,0:T(4,128)(2,1)}, bf16[32,2,512,128]{3,2,1,0:T(8,128)(2,1)S(1)}, bf16[4,1024,512]{2,1,0:T(8,128)(2,1)S(1)}) custom-call(bf16[256,4,128]{2,1,0:T(4,128)(2,1)} %q_own.1, bf16[512,4096]{1,0:T(8,128)(2,1)} %w_ref.1, bf16[256,1,4096,128]{3,2,1,0:T(8,128)(2,1)} %k_ref.5, bf16[256,1,4096,128]{3,2,1,0:T(8,128)(2,1)} %v_ref.5), custom_call_target="tpu_custom_call" | custom-call | tf_op jit(solution)/shard_map/spread/pallas_call | solution.py:76
  7.5 17.4 %attn.1 = (bf16[16,32,128]{2,1,0:T(8,128)(2,1)S(1)}, f32[3,512,128]{2,1,0:T(8,128)S(1)}, f32[32,16,128]{2,1,0:T(8,128)S(1)}) custom-call(s32[256]{0:T(256)} %len_ref.3, bf16[256,4,128]{2,1,0:T(4,128)(2,1)} %q_own.1, bf16[4,64,4,128]{3,2,1,0:T(4,128)(2,1)} %get-tuple-element.11.q_recv, bf16[32,2,512,128]{3,2,1,0:T(8,128)(2,1)S(1)} %get-tuple-element.12.pre, ...), custom_call_target="tpu_custom_call" | custom-call | tf_op jit(solution)/shard_map/attn/pallas_call | solution.py:278
  25.0 35.2 %tail.1 = bf16[256,512]{1,0:T(8,128)(2,1)S(1)} custom-call(s32[256]{0:T(256)} %len_ref.3, bf16[16,32,128]{2,1,0:T(8,128)(2,1)S(1)} %get-tuple-element.13.o1_ref, f32[3,512,128]{2,1,0:T(8,128)S(1)} %get-tuple-element.14.st_ref, f32[32,16,128]{2,1,0:T(8,128)S(1)} %get-tuple-element.15.qt, bf16[4,1024,512]{2,1,0:T(8,128)(2,1)S(1)} %get-tuple-element.16.wv, ...), custom_call_target="tpu_custom_call" | custom-call | tf_op jit(solution)/shard_map/tail/pallas_call | solution.py:479
  60.1 0.7 %copy.7 = bf16[256,512]{1,0:T(8,128)(2,1)} copy(bf16[256,512]{1,0:T(8,128)(2,1)S(1)} %tail.1) | data formatting | bytes 524288

commit v2 on v1

--- a/solution.py
+++ b/solution.py
@@ -9,17 +9,12 @@
 from jax.sharding import PartitionSpec as P
 
 R = 64
-R1 = 32
-R2 = R - R1
-K2 = 4
 T = 512
 HT = T // 2
 U = 8
 NG = 7
-NG2 = 6
-G2 = R2 * K2 // U
-G1 = R1 // U
-PRE_LIMIT = 40 * 2**20
+G1 = R // U
+PRE_LIMIT = 36 * 2**20
 H = 16
 D = 128
 C = (D ** -0.5) * math.log2(math.e)
@@ -64,7 +59,7 @@
         cps.append(pltpu.make_async_copy(w_ref.at[:, pl.ds(here, 512)], mine, wsem.at[j]))
     for c in cps:
         c.start()
-    lax.fori_loop(0, R1, load, 0)
+    lax.fori_loop(0, R, load, 0)
     for c in cps:
         c.wait()
     pltpu.make_async_copy(pre_ref, pre_ref, psem).wait()
@@ -75,7 +70,7 @@
     dma = pltpu.SemaphoreType.DMA
     return pl.pallas_call(
         spread_kernel,
-        out_shape=(pltpu.HBM((4, R, 4, D), BF16), pltpu.VMEM((R1, 2, T, D), BF16),
+        out_shape=(pltpu.HBM((4, R, 4, D), BF16), pltpu.VMEM((R, 2, T, D), BF16),
                    pltpu.VMEM((4, 1024, 512), BF16)),
         in_specs=[any_] * 4, out_specs=(any_,) + (pl.BlockSpec(memory_space=pltpu.VMEM),) * 2,
         scratch_shapes=[dma((3,)), dma((3,)), dma((4,)), dma((4,)), dma((4,)), dma],
@@ -122,7 +117,7 @@
     return mn, l0 * a + l * c, a0 * a + acc * c
 
 
-def attn_kernel(len_ref, q_own, q_recv, pre, k_ref, v_ref, o_ref, st_ref, q2_ref,
+def attn_kernel(len_ref, q_own, q_recv, pre, k_ref, v_ref, o_ref,
                 qv, q32, kv, sbuf, pbuf, mbuf, lbuf, o32, l32, m32, oi, li, mi, rows, tbl, qsem, sem):
     base = lax.axis_index('dup') * R
     me = lax.axis_index('dup')
@@ -131,12 +126,9 @@
     for c in qcp:
         c.start()
 
-    def first_tile(row):
-        return jnp.where(row < R1, 1, K2)
-
     def count(i, c):
         cnt, n = c
-        items = jnp.maximum((len_ref[base + i] + T - 1) // T - first_tile(i), 0)
+        items = jnp.maximum((len_ref[base + i] + T - 1) // T - 1, 0)
         rows[cnt] = i
         return cnt + jnp.where(items > 0, 1, 0), n + items
 
@@ -156,7 +148,7 @@
             tbl[2, b * U + u] = t
             done = jnp.logical_and((tile + 1) * T >= length, live)
             k = jnp.where(done, k + 1, k)
-            tile = jnp.where(done, first_tile(rows[k]), tile + 1)
+            tile = jnp.where(done, 1, tile + 1)
         return k, tile
 
     def issue(b):
@@ -175,16 +167,15 @@
         pltpu.make_async_copy(kv.at[b], kv.at[b], sem.at[b]).wait()
 
     z = jnp.int32(0)
-    pst = lax.fori_loop(0, jnp.minimum(3, ng), fetch_group, (z, first_tile(rows[0])))
+    pst = lax.fori_loop(0, jnp.minimum(3, ng), fetch_group, (z, jnp.int32(1)))
 
     for dst, val in ((m32, NEG), (l32, 0.0), (o32, 0.0), (mi, NEG), (li, 0.0), (oi, 0.0)):
-        dst[pl.ds(R1 * H, R2 * H + H), :] = jnp.full((R2 * H + H, D), val, F32)
+        dst[pl.ds(R * H, H), :] = jnp.full((H, D), val, F32)
     for c in qcp:
         c.wait()
     for s in range(4):
         q32[0:R, 4 * s:4 * s + 4, :] = qv[s].astype(F32)
 
-    q2_ref[...] = q32[R1:R]
     pst = lax.fori_loop(jnp.minimum(3, ng), jnp.minimum(NG, ng), fetch_group, pst)
 
     pos = _positions()
@@ -248,7 +239,7 @@
         for u in range(U):
             row = jnp.where(g - 1 < ng, tbl[0, bp * U + u], R)
             at = pl.ds(pl.multiple_of(row * H, H), H)
-            first = tbl[2, bp * U + u] == first_tile(row)
+            first = tbl[2, bp * U + u] == 1
             state = tuple(jnp.where(first, src[at, :], val) for src, val in zip((mi, li, oi), state))
             state = _merge(state, mbuf[oth, u], lbuf[oth, u], accs[u])
             for dst, val in zip((m32, l32, o32), state):
@@ -266,10 +257,8 @@
 
     state = (jnp.full((H, D), NEG, F32), jnp.ones((H, D), F32), jnp.zeros((H, D), F32))
     lax.fori_loop(0, (ng + 1) // 2, body, (pst, state))
-    for i, src in enumerate((m32, l32, o32)):
-        st_ref[i] = src[pl.ds(R1 * H, R2 * H), :]
     for h in range(H):
-        o_ref[h] = (o32[pl.ds(h, R1, stride=H), :] / l32[pl.ds(h, R1, stride=H), :]).astype(BF16)
+        o_ref[h] = (o32[pl.ds(h, R, stride=H), :] / l32[pl.ds(h, R, stride=H), :]).astype(BF16)
 
 
 def attention(q_own, q_recv, pre, k, v, lens):
@@ -277,9 +266,9 @@
     dma = pltpu.SemaphoreType.DMA
     return pl.pallas_call(
         attn_kernel,
-        out_shape=(pltpu.VMEM((H, R1, D), BF16), pltpu.VMEM((3, R2 * H, D), F32), pltpu.VMEM((R2, H, D), F32)),
+        out_shape=pltpu.VMEM((H, R, D), BF16),
         in_specs=[pl.BlockSpec(memory_space=pltpu.SMEM), any_, any_, pl.BlockSpec(memory_space=pltpu.VMEM), any_, any_],
-        out_specs=(pl.BlockSpec(memory_space=pltpu.VMEM),) * 3,
+        out_specs=pl.BlockSpec(memory_space=pltpu.VMEM),
         scratch_shapes=[
             pltpu.VMEM((4, R, 4, D), BF16), pltpu.VMEM((R + 1, H, D), F32),
             pltpu.VMEM((NG, U, 2, T, D), BF16),
@@ -294,9 +283,8 @@
     )(lens, q_own, q_recv, pre, k, v)
 
 
-def tail_kernel(len_ref, o1_ref, st_ref, qt, wv, k_ref, v_ref, y_ref,
-                st, kv, sbuf, pbuf, mbuf, lbuf, o2v, oc, part, r1a, r1b, r2a, r2b,
-                sem, oss, osr, s1s, s1a, s1b, s2s, s2a, s2b):
+def tail_kernel(o1_ref, wv, y_ref, oc, part, r1a, r1b, r2a, r2b,
+                oss, osr, s1s, s1a, s1b, s2s, s2a, s2b):
     me = lax.axis_index('dup')
     kvi = lax.axis_index('kv')
     core = lax.rem(me, 2)
@@ -305,23 +293,8 @@
     mate = me + 1 - 2 * core
     far = lax.rem(me + 2, 4)
     to_mate, to_x, to_y = {'dup': mate}, {'dup': far}, {'kv': okv}
-    base = me * R + R1
-    RR = R1
-
-    def fetch_group(g):
-        b = lax.rem(g, NG2)
-        for u in range(U):
-            i = g * U + u
-            for j, src in enumerate((k_ref, v_ref)):
-                pltpu.make_async_copy(src.at[base + i // K2, 0, pl.ds(pl.multiple_of(lax.rem(i, K2) * T, T), T), :],
-                                      kv.at[b, u, j], sem.at[b]).start()
-
-    def wait_group(g):
-        b = lax.rem(g, NG2)
-        pltpu.make_async_copy(kv.at[b], kv.at[b], sem.at[b]).wait()
-
-    for g in range(2):
-        fetch_group(jnp.int32(g))
+    RR = R
+
     _enter([to_mate, to_x, to_y])
 
     def exchange(p, src):
@@ -334,10 +307,6 @@
     o_x, o_m = exchange(0, o1_ref)
     oc[0, me] = o1_ref[pl.ds(x * 8, 8)]
     order = (okv * 2 + ox, kvi * 2 + ox, okv * 2 + x, kvi * 2 + x)
-    for g in range(2, NG2):
-        fetch_group(jnp.int32(g))
-
-    pos = _positions()
     sends = []
 
     def forward(p, o_x):
@@ -402,101 +371,35 @@
                     row = pl.multiple_of(X * 2 * R + c * R + p * RR, RR)
                     y_ref[pl.ds(row, RR), half * 256:half * 256 + 256] = val[c * RR:(c + 1) * RR]
 
-    def scores(g, oth):
-        b = lax.rem(g, NG2)
-        for u in range(U):
-            sbuf[oth, u] = _scores(qt[(g * U + u) // K2], kv.at[b, u, 0])
-
-    def stage(g, cur, state, qk=True, sm=True, pv=True):
-        oth = 1 - cur
-        if qk:
-            wait_group(g + 1)
-        accs = None
-        bp = lax.rem(g - 1 + NG2, NG2)
-        if pv:
-            accs = [_weighted(pbuf[oth, u], kv.at[bp, u, 1]) for u in range(U)]
-        if qk:
-            scores(g + 1, oth)
-        if sm:
-            for u in range(U):
-                i = g * U + u
-                rem = len_ref[base + i // K2] - lax.rem(i, K2) * T
-                _softmax(sbuf[cur, u], pos, rem, pbuf.at[cur, u], mbuf.at[cur, u], lbuf.at[cur, u])
-        if pv:
-            for u in range(U):
-                i = (g - 1) * U + u
-                at = pl.ds(pl.multiple_of((i // K2) * H, H), H)
-                if u % K2 == 0:
-                    state = (st_ref[0, at, :], st_ref[1, at, :], st_ref[2, at, :])
-                state = _merge(state, mbuf[oth, u], lbuf[oth, u], accs[u])
-                if u % K2 == K2 - 1:
-                    st[0, at, :] = state[1]
-                    st[1, at, :] = state[2]
-        if qk and pv:
-            @pl.when(g - 1 + NG2 < G2)
-            def _():
-                fetch_group(g - 1 + NG2)
-        return state
-
-    def pair(h, state):
-        return stage(2 * h + 2, 0, stage(2 * h + 1, 1, state))
-
-    wait_group(jnp.int32(0))
-    scores(jnp.int32(0), 0)
-    state = (jnp.zeros((H, D), F32),) * 3
-    stage(jnp.int32(0), 0, state, pv=False)
-    last = (G2 - 2) // 2
-    state = lax.fori_loop(0, 1, pair, state)
+    o_m.wait()
+    multiply(0, (0,))
     fwd = forward(0, o_x)
-    state = lax.fori_loop(1, 2, pair, state)
     fwd.wait()
-    o_m.wait()
-    multiply(0, (0, 1))
-    state = lax.fori_loop(2, last, pair, state)
-    stage(jnp.int32(G2 - 1), 1, state, qk=False)
-    stage(jnp.int32(G2), 0, state, qk=False, sm=False)
-    for h in range(H):
-        o2v[h] = (st[1, pl.ds(h, R2, stride=H), :] / st[0, pl.ds(h, R2, stride=H), :]).astype(BF16)
-    o_x, o_m = exchange(1, o2v)
-    oc[1, me] = o2v[pl.ds(x * 8, 8)]
-    o_m.wait()
-    multiply(1, (0,))
+    multiply(0, (1,))
     second(0)
-    fwd = forward(1, o_x)
     finish(0)
-    fwd.wait()
-    multiply(1, (1,))
-    second(1)
-    finish(1)
     for c in sends:
         c.wait_send()
 
 
-def tail(lens, o1, st, q2, wv, k, v):
-    any_ = pl.BlockSpec(memory_space=pltpu.HBM)
+def tail(o1, wv):
     dma = pltpu.SemaphoreType.DMA
-    M = 2 * R1
+    M = 2 * R
     return pl.pallas_call(
         tail_kernel,
         out_shape=jax.ShapeDtypeStruct((256, 512), BF16),
-        in_specs=[pl.BlockSpec(memory_space=pltpu.SMEM)] + [pl.BlockSpec(memory_space=pltpu.VMEM)] * 4 + [any_] * 2, out_specs=pl.BlockSpec(memory_space=pltpu.VMEM),
+        in_specs=[pl.BlockSpec(memory_space=pltpu.VMEM)] * 2, out_specs=pl.BlockSpec(memory_space=pltpu.VMEM),
         scratch_shapes=[
-            pltpu.VMEM((2, R2 * H, D), F32),
-            pltpu.VMEM((NG2, U, 2, T, D), BF16),
-            pltpu.VMEM((2, U, 2 * H, HT), F32), pltpu.VMEM((2, U, 2 * H, HT), BF16),
-            pltpu.VMEM((2, U, H, D), F32), pltpu.VMEM((2, U, H, D), F32),
-            pltpu.VMEM((H, R2, D), BF16),
-            pltpu.VMEM((2, 4, 8, R1, D), BF16),
-            pltpu.VMEM((2, 2, 4, 2, M, 256), F32),
-            pltpu.VMEM((2, 2, 2, M, 256), F32), pltpu.VMEM((2, 2, 2, M, 256), F32),
-            pltpu.VMEM((2, 2, M, 256), F32), pltpu.VMEM((2, 2, M, 256), F32),
-            dma((NG2,)), dma((2, 3)), dma((2, 3)),
-            dma((2, 2, 4)), dma((2, 2, 2)), dma((2, 2, 2)),
-            dma((2, 2, 2)), dma((2, 2)), dma((2, 2)),
+            pltpu.VMEM((1, 4, 8, R, D), BF16),
+            pltpu.VMEM((1, 2, 4, 2, M, 256), F32),
+            pltpu.VMEM((1, 2, 2, M, 256), F32), pltpu.VMEM((1, 2, 2, M, 256), F32),
+            pltpu.VMEM((1, 2, M, 256), F32), pltpu.VMEM((1, 2, M, 256), F32),
+            dma((1, 3)), dma((1, 3)), dma((1, 2, 4)), dma((1, 2, 2)), dma((1, 2, 2)),
+            dma((1, 2, 2)), dma((1, 2)), dma((1, 2)),
         ],
         compiler_params=pltpu.CompilerParams(collective_id=1, has_side_effects=True, vmem_limit_bytes=48 * 2**20),
         name='tail',
-    )(lens, o1, st, q2, wv, k, v)
+    )(o1, wv)
 
 
 def solution(mesh):
@@ -504,8 +407,8 @@
         q, lens, w = (pltpu.with_memory_space_constraint(a, pltpu.HBM) for a in (q, lens, w))
         q_recv, pre, wv = spread(q, w, k, v)
         q_recv = pltpu.with_memory_space_constraint(q_recv, pltpu.HBM)
-        o1, st, q2 = attention(q, q_recv, pre, k, v, lens)
-        return tail(lens, o1, st, q2, wv, k, v)
+        o1 = attention(q, q_recv, pre, k, v, lens)
+        return tail(o1, wv)
 
     return jax.shard_map(
         per_device,

time: 61 us -> 61 us (level)
    pallas_call x1, Pallas kernels: 35.2 us -> 22.7 us  [tail(): pl.pallas_call(tail_kernel, out_shape=jax.ShapeDtypeStruct((256, 512), BF...]
    pallas_call x1, Pallas kernels: 17.4 us -> 27.1 us  [attention(): pl.pallas_call(attn_kernel, out_shape=pltpu.VMEM((H, R, D), BF16), in_spe...]
    pallas_call x1, Pallas kernels: 7.52 us -> 9.98 us  [spread(): pl.pallas_call(spread_kernel, out_shape=(pltpu.HBM((4, R, 4, D), BF16), p...]
where the time goes in v2:
time: 61 us; the launch traced here: 60.5 us
  Pallas kernels  59.7 us (98%)
  local copies, waits for them, and re-layouts  0.71 us (1%)
    pallas_call x1, Pallas kernels, attention(): pl.pallas_call(attn_kernel, out_shape=pltpu.VMEM((H, R, D), BF16), in_spe...  27.1 us
    pallas_call x1, Pallas kernels, tail(): pl.pallas_call(tail_kernel, out_shape=jax.ShapeDtypeStruct((256, 512), BF...  22.7 us
    pallas_call x1, Pallas kernels, spread(): pl.pallas_call(spread_kernel, out_shape=(pltpu.HBM((4, R, 4, D), BF16), p...  9.98 us

profile of v2, /device:TPU:0, one launch (start us, length us, event | category | flops | bytes accessed | tf_op | source)
XLA Modules:
  0.0 60.5 jit_solution(11067030371709191304)
XLA Ops:
  0.0 10.0 %spread.1 = (bf16[4,64,4,128]{3,2,1,0:T(4,128)(2,1)}, bf16[64,2,512,128]{3,2,1,0:T(8,128)(2,1)S(1)}, bf16[4,1024,512]{2,1,0:T(8,128)(2,1)S(1)}) custom-call(bf16[256,4,128]{2,1,0:T(4,128)(2,1)} %q_own.1, bf16[512,4096]{1,0:T(8,128)(2,1)} %w_ref.1, bf16[256,1,4096,128]{3,2,1,0:T(8,128)(2,1)} %k_ref.3, bf16[256,1,4096,128]{3,2,1,0:T(8,128)(2,1)} %v_ref.3), custom_call_target="tpu_custom_call" | custom-call | tf_op jit(solution)/shard_map/spread/pallas_call | solution.py:71
  10.0 27.1 %attn.1.o1_ref = bf16[16,64,128]{2,1,0:T(8,128)(2,1)S(1)} custom-call(s32[256]{0:T(256)} %len_ref.1, bf16[256,4,128]{2,1,0:T(4,128)(2,1)} %q_own.1, bf16[4,64,4,128]{3,2,1,0:T(4,128)(2,1)} %get-tuple-element.8.q_recv, bf16[64,2,512,128]{3,2,1,0:T(8,128)(2,1)S(1)} %get-tuple-element.9.pre, bf16[256,1,4096,128]{3,2,1,0:T(8,128)(2,1)} %k_ref.3, ...), custom_call_target="tpu_custom_call" | custom-call | tf_op jit(solution)/shard_map/attn/pallas_call | solution.py:267
  37.1 22.7 %tail.1 = bf16[256,512]{1,0:T(8,128)(2,1)S(1)} custom-call(bf16[16,64,128]{2,1,0:T(8,128)(2,1)S(1)} %attn.1.o1_ref, bf16[4,1024,512]{2,1,0:T(8,128)(2,1)S(1)} %get-tuple-element.10.wv), custom_call_target="tpu_custom_call" | custom-call | tf_op jit(solution)/shard_map/tail/pallas_call | solution.py:388
  59.8 0.7 %copy.7 = bf16[256,512]{1,0:T(8,128)(2,1)} copy(bf16[256,512]{1,0:T(8,128)(2,1)S(1)} %tail.1) | data formatting | bytes 524288
